TPU v7x, 32 devices: a whole 2x2x4 slice. The times are simulated.
32 devices in a mesh: clip: 2 (over y), tm: 4 (over z), space: 2 (over x), chan: 2 (over core).
Axes of the slice: x: 2, y: 2, z: 4, core: 2. Of those that a mesh axis runs over, the one named last changes fastest.
Arguments:
- features: bfloat16 [16, 8, 90, 256], P(('clip', 'tm'), 'space'), parts along dimension 0, may hold values from -700 to 700
- hidden: bfloat16 [16, 8, 90, 256], P(('clip', 'tm'), 'space'), parts along dimension 0, may hold values from -700 to 700
- cotangent: bfloat16 [16, 8, 90, 256], P(('clip', 'tm'), 'space'), parts along dimension 0, may hold values from -6 to 6
- kernel_one: bfloat16 [256, 3, 3, 3, 256], P(None, None, None, None, 'chan'), may hold values from -0.078125 to 0.078125
- kernel_two: bfloat16 [256, 3, 3, 3, 256], P(None, None, None, None, 'chan'), may hold values from -0.078125 to 0.078125
- gains: float32 [2, 256], replicated, may hold values from 0.25 to 1.75
Outputs:
- feature_grad: bfloat16 [16, 8, 90, 256], P(('clip', 'tm'), 'space', None, 'chan'), parts along dimension 0
- delta_one: float32 [512, 3, 3, 3, 256], P(('clip', 'tm', 'space'), None, None, None, 'chan'), parts along dimension 0
- delta_two: float32 [512, 3, 3, 3, 256], P(('clip', 'tm', 'space'), None, None, None, 'chan'), parts along dimension 0
- gain_grads: float32 [4, 256], P('clip', 'chan'), parts along dimension 0
There are 2 independent parts, one for each index of `clip`. A program takes and returns all parts, laid end to end along the dimension named above; an argument that names none is the same for every part. Nothing has to cross between parts.
All inputs are finite; a program needn't handle non-finite values.
Results may differ from a plain program's by a relative error of at most 0.005.
Values may be sent and summed in bfloat16 or wider, within the bound.
A program may use at most 128 MiB of HBM per device.

v0:
```python
import jax
import jax.numpy as jnp
from jax import lax
from jax.sharding import PartitionSpec as P

GROUPS = 32
epsilon = 1e-06


def extended_2(cells, sides, width):
    for axis, dim in sides:
        count = lax.axis_size(axis)
        ends = count - 1
        head = lax.slice_in_dim(cells, 0, width, axis=dim)
        tail = lax.slice_in_dim(cells, cells.shape[dim] - width, cells.shape[dim], axis=dim)
        cells = jnp.concatenate(
            [
                lax.ppermute(tail, axis, [(i, (i + 1) % count) for i in range(ends)]),
                cells,
                lax.ppermute(head, axis, [((i + 1) % count, i) for i in range(ends)]),
            ],
            axis=dim,
        )
    return cells


def passed_along(block, axis, distance):
    devices = range(lax.axis_size(axis))
    route = [(i - distance, i) for i in devices if i - distance in devices]
    return lax.ppermute(block, axis, route)


def clip_totals(values):
    return lax.psum(values, ("tm", "space"))


def statistics(total, square, members, per):
    mean = jnp.sum(total.reshape(-1, per), axis=1) / members
    spread = jnp.sum(square.reshape(-1, per), axis=1) / members - mean * mean
    scale = lax.rsqrt(spread + epsilon)
    return (jnp.repeat(mean, per), jnp.repeat(scale, per))


def norm_back(upstream, centred, scaled, gain, scale, members, per):
    gate = jax.nn.sigmoid(scaled)
    slope = upstream * gate * (1.0 + scaled * (1.0 - gate))
    totals = clip_totals(
        jnp.stack([jnp.sum(slope, axis=(0, 1, 2)), jnp.sum(slope * centred, axis=(0, 1, 2))])
    )
    first = jnp.repeat(jnp.sum((gain * totals[0]).reshape(-1, per), axis=1), per) / members
    second = jnp.repeat(jnp.sum((gain * totals[1]).reshape(-1, per), axis=1), per) / members
    return (scale * (slope * gain - first - centred * second), totals[1])


def extend(grad):
    edged = extended_2(grad, (("space", 1),), 1)
    later = passed_along(edged, "tm", -1)
    joined = jnp.concatenate([edged, later], axis=0)
    return jnp.pad(joined, ((0, 0), (0, 0), (1, 1), (0, 0)))


def tap_stack(extended, frames, height, width):
    pieces = []
    for frame_tap in range(3):
        for row_tap in range(3):
            for col_tap in range(3):
                pieces.append(
                    extended[
                        2 - frame_tap : 2 - frame_tap + frames,
                        2 - row_tap : 2 - row_tap + height,
                        2 - col_tap : 2 - col_tap + width,
                    ]
                )
    stacked = jnp.stack(pieces, axis=3)
    return stacked.reshape(frames * height * width, 27, extended.shape[3])


def kernel_term(flat_active, taps):
    depth = taps.shape[2]
    flat_taps = taps.reshape(taps.shape[0], 27 * depth)

    def term(start, count):
        product = lax.dot_general(
            flat_active, flat_taps, (((0,), (0,)), ((), ())), preferred_element_type=jnp.float32
        )
        return product.reshape(count, 3, 3, 3, depth)

    return term


def layer_back(active, upstream, kernel, half):
    frames, height, width, channels = active.shape
    taps = tap_stack(extend(upstream), frames, height, width)
    flat_active = active.reshape(frames * height * width, channels)
    term = kernel_term(flat_active, taps)
    partial_grad = lax.dot_general(
        taps,
        kernel.reshape(channels, 27, half),
        (((1, 2), (1, 2)), ((), ())),
        preferred_element_type=jnp.float32,
    )
    back = lax.psum_scatter(
        partial_grad.reshape(frames, height, width, channels),
        "chan",
        scatter_dimension=3,
        tiled=True,
    )
    return (term, back)


def shards(features, hidden, cotangent, kernel_one, kernel_two, gains):
    frames, height, width, channels = features.shape
    half = kernel_one.shape[4]
    per = channels // GROUPS
    offset = lax.axis_index("chan") * half
    members = float(frames * height * width * per * lax.axis_size("tm") * lax.axis_size("space"))
    share = channels // (lax.axis_size("tm") * lax.axis_size("space"))

    def own(field):
        return lax.dynamic_slice_in_dim(field, offset, half, field.ndim - 1)

    field_one = features.astype(jnp.float32)
    field_two = hidden.astype(jnp.float32)
    totals = clip_totals(
        jnp.stack(
            [
                jnp.sum(field_one, axis=(0, 1, 2)),
                jnp.sum(field_one * field_one, axis=(0, 1, 2)),
                jnp.sum(field_two, axis=(0, 1, 2)),
                jnp.sum(field_two * field_two, axis=(0, 1, 2)),
            ]
        )
    )
    mean_one, scale_one = statistics(totals[0], totals[1], members, per)
    mean_two, scale_two = statistics(totals[2], totals[3], members, per)
    centred_one = (field_one - mean_one) * scale_one
    scaled_one = centred_one * gains[0]
    active_one = (scaled_one * jax.nn.sigmoid(scaled_one)).astype(jnp.bfloat16)
    centred_two = (field_two - mean_two) * scale_two
    scaled_two = centred_two * gains[1]
    active_two = (scaled_two * jax.nn.sigmoid(scaled_two)).astype(jnp.bfloat16)
    upstream_two = own(cotangent)
    term_two, back_two = layer_back(active_two, upstream_two, kernel_two, half)
    grad_two, weighted_two = norm_back(
        back_two, own(centred_two), own(scaled_two), own(gains[1]), own(scale_two), members, per
    )
    grad_hidden = grad_two.astype(jnp.bfloat16)
    term_one, back_one = layer_back(active_one, grad_hidden, kernel_one, half)
    start = jnp.int32(0)
    combined = lax.psum_scatter(
        jnp.stack(
            [
                term_one(start, lax.axis_size(("tm", "space")) * share),
                term_two(start, lax.axis_size(("tm", "space")) * share),
            ],
            axis=1,
        ),
        ("tm", "space"),
        scatter_dimension=0,
        tiled=True,
    )
    delta_one = combined[:, 0]
    delta_two = combined[:, 1]
    grad_one, weighted_one = norm_back(
        back_one, own(centred_one), own(scaled_one), own(gains[0]), own(scale_one), members, per
    )
    feature_grad = (own(cotangent).astype(jnp.float32) + grad_one).astype(jnp.bfloat16)
    return (feature_grad, delta_one, delta_two, jnp.stack([weighted_one, weighted_two]))


def solution(mesh):
    placed = (
        P(("clip", "tm"), "space", None, None),
        P(("clip", "tm"), "space", None, None),
        P(("clip", "tm"), "space", None, None),
        P(None, None, None, None, "chan"),
        P(None, None, None, None, "chan"),
        P(),
    )
    return jax.shard_map(
        shards,
        mesh=mesh,
        in_specs=placed,
        out_specs=(
            P(("clip", "tm"), "space", None, "chan"),
            P(("clip", "tm", "space"), None, None, None, "chan"),
            P(("clip", "tm", "space"), None, None, None, "chan"),
            P("clip", "chan"),
        ),
        check_vma=False,
    )
```

profile of v0, /device:TPU:0, one launch (start us, length us, event | category | flops | bytes accessed | tf_op | source)
XLA Modules:
  0.0 289.6 jit_solution(4879320679843734137)
XLA Ops:
  7.2 1.1 constant_dynamic-slice_fusion.2
  8.4 4.9 %collective-permute-start = (bf16[2,1,90,128]{3,2,1,0:T(8,128)(2,1)S(1)}, bf16[2,1,90,128]{3,2,1,0:T(8,128)(2,1)S(1)}, u32[]{:S(2)}, u32[]{:S(2)}) collective-permute-start(bf16[2,1,90,128]{3,2,1,0:T(8,128)(2,1)S(1)} %get-tuple-element.41), channel_id=1, source_target_pairs={{0,2},{1,3},{4,6},{5,7},{8,10},{9,11},{12,14},{13,15},{16,18},{17,... | collective-permute-start | bytes 138248 | tf_op jit(solution)/shard_map/ppermute | solution.py:18
  13.3 1.3 collective-permute-start.1
  15.1 4.2 %collective-permute-done.1 = bf16[2,1,90,128]{3,2,1,0:T(8,128)(2,1)S(1)} collective-permute-done((bf16[2,1,90,128]{3,2,1,0:T(8,128)(2,1)S(1)}, bf16[2,1,90,128]{3,2,1,0:T(8,128)(2,1)S(1)}, u32[]{:S(2)}, u32[]{:S(2)}) %collective-permute-start.1) | collective-permute-done | bytes 46112 | tf_op jit(solution)/shard_map/ppermute | solution.py:20
  19.3 1.3 collective-permute-start.2
  20.6 7.9 %collective-permute-done.2 = bf16[2,6,90,128]{3,2,1,0:T(8,128)(2,1)S(1)} collective-permute-done((bf16[2,6,90,128]{3,2,1,0:T(8,128)(2,1)S(1)}, bf16[2,6,90,128]{3,2,1,0:T(8,128)(2,1)S(1)}, u32[]{:S(2)}, u32[]{:S(2)}) %collective-permute-start.2) | collective-permute-done | bytes 276512 | tf_op jit(solution)/shard_map/ppermute | solution.py:30
  30.3 2.3 copy-done.3
  32.7 2.5 convolution_bitcast_fusion.2
  35.6 18.1 %psum.21 = f32[4,256]{1,0:T(4,128)S(1)} all-reduce(f32[4,256]{1,0:T(4,128)S(1)} %pad_maximum_fusion.8), channel_id=1, replica_groups=mesh['clip'=2,'tm'=4,'space'=2,'chan'=2] {'tm','space'}, use_global_device_ids=true, to_apply=%region_4.0 | all-reduce | flops 1024 | bytes 8192 | tf_op jit(solution)/shard_map/psum | solution.py:34
  54.6 1.0 multiply_convert_fusion
  55.6 1.2 fusion.37
  56.8 18.2 %psum.22 = f32[2,128]{1,0:T(2,128)S(1)} all-reduce(f32[2,128]{1,0:T(2,128)S(1)} %pad_maximum_fusion.9), channel_id=1, replica_groups=mesh['clip'=2,'tm'=4,'space'=2,'chan'=2] {'tm','space'}, use_global_device_ids=true, to_apply=%region_12.13 | all-reduce | flops 256 | bytes 2048 | tf_op jit(solution)/shard_map/psum | solution.py:34
  75.9 2.9 collective-permute-start.3
  78.8 1.3 collective-permute-start.4
  80.5 4.3 %collective-permute-done.4 = bf16[2,1,90,128]{3,2,1,0:T(8,128)(2,1)S(1)} collective-permute-done((bf16[2,1,90,128]{3,2,1,0:T(8,128)(2,1)S(1)}, bf16[2,1,90,128]{3,2,1,0:T(8,128)(2,1)S(1)}, u32[]{:S(2)}, u32[]{:S(2)}) %collective-permute-start.4) | collective-permute-done | bytes 46112 | tf_op jit(solution)/shard_map/ppermute | solution.py:20
  84.8 1.3 collective-permute-start.5
  86.9 6.5 %collective-permute-done.5 = bf16[2,6,90,128]{3,2,1,0:T(8,128)(2,1)S(1)} collective-permute-done((bf16[2,6,90,128]{3,2,1,0:T(8,128)(2,1)S(1)}, bf16[2,6,90,128]{3,2,1,0:T(8,128)(2,1)S(1)}, u32[]{:S(2)}, u32[]{:S(2)}) %collective-permute-start.5) | collective-permute-done | bytes 276512 | tf_op jit(solution)/shard_map/ppermute | solution.py:30
  95.6 1.6 fusion
  99.3 4.6 %copy.72 = bf16[2,4,90,27,128]{4,3,2,1,0:T(8,128)(2,1)S(1)} copy(bf16[2,4,90,27,128]{4,2,3,1,0:T(8,128)(2,1)} %copy-done.3) | data formatting | bytes 9953280 | tf_op jit(solution)/shard_map/stack | solution.py:74
  103.9 7.3 %copy.111 = bf16[90,8,27,128]{3,1,2,0:T(8,128)(2,1)} copy(bf16[90,8,27,128]{3,2,1,0:T(8,128)(2,1)S(1)} %bitcast.258) | data formatting | bytes 9953280
  111.2 7.9 %copy.73 = bf16[3456,720]{1,0:T(8,128)(2,1)} copy(bf16[3456,720]{0,1:T(8,128)(2,1)} %bitcast.262) | data formatting | bytes 9953280 | tf_op jit(solution)/shard_map/dot_general | solution.py:83
  119.1 6.0 %convolution_bitcast_fusion = f32[256,1,3,3,3,128]{5,0,4,3,2,1:T(8,128)} fusion(bf16[3,3,3,128,720]{4,3,2,1,0:T(8,128)(2,1)} %bitcast.260, bf16[720,256,1,1,1]{1,0,2,3,4:T(8,128)(2,1)S(1)} %reshape.335), kind=kOutput, calls=%fused_computation.5 | convolution fusion | flops 1274019840 | bytes 8884224 | tf_op jit(solution)/shard_map/dot_general | solution.py:83
  125.1 5.8 %copy.69 = bf16[2,4,90,27,128]{4,3,2,1,0:T(8,128)(2,1)S(1)} copy(bf16[2,4,90,27,128]{4,2,1,0,3:T(8,128)(2,1)} %copy-done.4) | data formatting | bytes 9953280 | tf_op jit(solution)/shard_map/stack | solution.py:74
  130.9 7.3 %copy.112 = bf16[90,8,27,128]{3,1,2,0:T(8,128)(2,1)} copy(bf16[90,8,27,128]{3,2,1,0:T(8,128)(2,1)S(1)} %bitcast.259) | data formatting | bytes 9953280
  138.2 8.0 %copy.70 = bf16[3456,720]{1,0:T(8,128)(2,1)} copy(bf16[3456,720]{0,1:T(8,128)(2,1)} %bitcast.263) | data formatting | bytes 9953280 | tf_op jit(solution)/shard_map/dot_general | solution.py:83
  146.2 4.3 %convolution_bitcast_fusion.1 = f32[256,1,3,3,3,128]{5,0,4,3,2,1:T(8,128)S(1)} fusion(bf16[3,3,3,128,720]{4,3,2,1,0:T(8,128)(2,1)} %bitcast.261, bf16[720,256,1,1,1]{1,0,2,3,4:T(8,128)(2,1)S(1)} %reshape.334), kind=kOutput, calls=%fused_computation.6 | convolution fusion | flops 1274019840 | bytes 8884224 | tf_op jit(solution)/shard_map/dot_general | solution.py:83
  150.5 3.4 %pad_maximum_fusion = f32[256,2,3,3,3,128]{5,0,4,3,2,1:T(8,128)} fusion(f32[256,1,3,3,3,128]{5,0,4,3,2,1:T(8,128)S(1)} %copy-done.2, f32[256,1,3,3,3,128]{5,0,4,3,2,1:T(8,128)S(1)} %convolution_bitcast_fusion.1), kind=kLoop, calls=%fused_computation | loop fusion | flops 1769472 | bytes 14155776 | tf_op jit(solution)/shard_map/stack | solution.py:151
  154.0 2.0 fusion.36
  156.0 18.2 %psum.23 = f32[2,128]{1,0:T(2,128)S(1)} all-reduce(f32[2,128]{1,0:T(2,128)S(1)} %pad_maximum_fusion.10), channel_id=1, replica_groups=mesh['clip'=2,'tm'=4,'space'=2,'chan'=2] {'tm','space'}, use_global_device_ids=true, to_apply=%region_18.19 | all-reduce | flops 256 | bytes 2048 | tf_op jit(solution)/shard_map/psum | solution.py:34
  175.0 1.1 add_convert_fusion
  177.5 103.5 %reduce-scatter.8.cloned.1.call-done = f32[32,2,3,3,3,128]{5,0,4,3,2,1:T(8,128)} async-done(((f32[256,2,3,3,3,128]{5,0,4,3,2,1:T(8,128)}), f32[32,2,3,3,3,128]{5,0,4,3,2,1:T(8,128)}) %reduce-scatter.8.cloned.1.call-update) | async-done | bytes 884752 | tf_op jit(solution)/shard_map/reduce_scatter | solution.py:150
  281.0 2.1 slice_bitcast_fusion
  (150 shorter events, 11.9 us)
Async XLA Ops:
  7.2 23.1 %copy-start = (bf16[256,3,3,3,128]{4,0,3,2,1:T(8,128)(2,1)S(1)}, bf16[256,3,3,3,128]{4,0,3,2,1:T(8,128)(2,1)}, u32[]{:S(2)}) copy-start(bf16[256,3,3,3,128]{4,0,3,2,1:T(8,128)(2,1)} %param.10) | copy-start | bytes 5308420
  7.2 48.4 %reduce-scatter.4.cloned.1.call-start = ((), (), s32[]{:S(2)}) async-start(), calls=%async_computation.3 | async-start | bytes 1179648 | tf_op jit(solution)/shard_map/reduce_scatter | solution.py:102
  8.4 6.6 %collective-permute-start = (bf16[2,1,90,128]{3,2,1,0:T(8,128)(2,1)S(1)}, bf16[2,1,90,128]{3,2,1,0:T(8,128)(2,1)S(1)}, u32[]{:S(2)}, u32[]{:S(2)}) collective-permute-start(bf16[2,1,90,128]{3,2,1,0:T(8,128)(2,1)S(1)} %get-tuple-element.41), channel_id=1, source_target_pairs={{0,2},{1,3},{4,6},{5,7},{8,10},{9,11},{12,14},{13,15},{16,18},{17,... | collective-permute-start | bytes 138248 | tf_op jit(solution)/shard_map/ppermute | solution.py:18
  13.3 6.0 %collective-permute-start.1 = (bf16[2,1,90,128]{3,2,1,0:T(8,128)(2,1)S(1)}, bf16[2,1,90,128]{3,2,1,0:T(8,128)(2,1)S(1)}, u32[]{:S(2)}, u32[]{:S(2)}) collective-permute-start(bf16[2,1,90,128]{3,2,1,0:T(8,128)(2,1)S(1)} %get-tuple-element.40), channel_id=1, source_target_pairs={{2,0},{3,1},{6,4},{7,5},{10,8},{11,9},{14,12},{15,13},{18,16},{19,... | collective-permute-start | bytes 138248 | tf_op jit(solution)/shard_map/ppermute | solution.py:20
  19.3 9.2 %collective-permute-start.2 = (bf16[2,6,90,128]{3,2,1,0:T(8,128)(2,1)S(1)}, bf16[2,6,90,128]{3,2,1,0:T(8,128)(2,1)S(1)}, u32[]{:S(2)}, u32[]{:S(2)}) collective-permute-start(bf16[2,6,90,128]{3,2,1,0:T(8,128)(2,1)S(1)} %constant_dynamic-update-slice_fusion), channel_id=1, source_target_pairs={{4,0},{8,4},{12,8},{5,1},{9,5},{13,9},{6,2},{10,6},{14,10},{7,3},{... | collective-permute-start | bytes 829448 | tf_op jit(solution)/shard_map/ppermute | solution.py:30
  30.3 2.3 copy-start.3
  30.3 4.9 %copy-start.7 = (bf16[2,4,90,256]{3,1,2,0:T(4,128)(2,1)S(1)}, bf16[2,4,90,256]{3,1,2,0:T(4,128)(2,1)}, u32[]{:S(2)}) copy-start(bf16[2,4,90,256]{3,1,2,0:T(4,128)(2,1)} %param.6) | copy-start | bytes 1105924
  32.7 2.7 copy-start.6
  32.7 21.9 %copy-start.9 = (f32[2,256]{1,0:T(2,128)S(1)}, f32[2,256]{1,0:T(2,128)}, u32[]{:S(2)}) copy-start(f32[2,256]{1,0:T(2,128)} %param.11) | copy-start | bytes 6148
  35.2 118.8 %reduce-scatter.6.cloned.1.call-start = ((), (), s32[]{:S(2)}) async-start(), calls=%async_computation.4 | async-start | bytes 1179648 | tf_op jit(solution)/shard_map/reduce_scatter | solution.py:102
  75.9 4.6 %collective-permute-start.3 = (bf16[2,1,90,128]{3,2,1,0:T(8,128)(2,1)S(1)}, bf16[2,1,90,128]{3,2,1,0:T(8,128)(2,1)S(1)}, u32[]{:S(2)}, u32[]{:S(2)}) collective-permute-start(bf16[2,1,90,128]{3,2,1,0:T(8,128)(2,1)S(1)} %get-tuple-element.38), channel_id=1, source_target_pairs={{0,2},{1,3},{4,6},{5,7},{8,10},{9,11},{12,14},{13,15},{16,18},{17,... | collective-permute-start | bytes 138248 | tf_op jit(solution)/shard_map/ppermute | solution.py:18
  78.8 6.0 %collective-permute-start.4 = (bf16[2,1,90,128]{3,2,1,0:T(8,128)(2,1)S(1)}, bf16[2,1,90,128]{3,2,1,0:T(8,128)(2,1)S(1)}, u32[]{:S(2)}, u32[]{:S(2)}) collective-permute-start(bf16[2,1,90,128]{3,2,1,0:T(8,128)(2,1)S(1)} %get-tuple-element.39), channel_id=1, source_target_pairs={{2,0},{3,1},{6,4},{7,5},{10,8},{11,9},{14,12},{15,13},{18,16},{19,... | collective-permute-start | bytes 138248 | tf_op jit(solution)/shard_map/ppermute | solution.py:20
  84.8 8.6 %collective-permute-start.5 = (bf16[2,6,90,128]{3,2,1,0:T(8,128)(2,1)S(1)}, bf16[2,6,90,128]{3,2,1,0:T(8,128)(2,1)S(1)}, u32[]{:S(2)}, u32[]{:S(2)}) collective-permute-start(bf16[2,6,90,128]{3,2,1,0:T(8,128)(2,1)S(1)} %pad_maximum_fusion.3), channel_id=1, source_target_pairs={{4,0},{8,4},{12,8},{5,1},{9,5},{13,9},{6,2},{10,6},{14,10},{7,3},{... | collective-permute-start | bytes 829448 | tf_op jit(solution)/shard_map/ppermute | solution.py:30
  94.2 1.5 copy-start.10
  95.2 2.3 copy-start.4
  95.6 3.1 %copy-start.8 = (bf16[2,4,90,256]{3,1,2,0:T(4,128)(2,1)S(1)}, bf16[2,4,90,256]{3,1,2,0:T(4,128)(2,1)}, u32[]{:S(2)}) copy-start(bf16[2,4,90,256]{3,1,2,0:T(4,128)(2,1)} %param.6) | copy-start | bytes 1105924
  97.5 1.6 copy-start.5
  98.5 182.5 %reduce-scatter.8.cloned.1.call-start = ((), (), s32[]{:S(2)}) async-start(), calls=%async_computation.5 | async-start | bytes 7962624 | tf_op jit(solution)/shard_map/reduce_scatter | solution.py:150
  146.2 4.3 %copy-start.2 = (f32[256,1,3,3,3,128]{5,0,4,3,2,1:T(8,128)S(1)}, f32[256,1,3,3,3,128]{5,0,4,3,2,1:T(8,128)}, u32[]{:S(2)}) copy-start(f32[256,1,3,3,3,128]{5,0,4,3,2,1:T(8,128)} %convolution_bitcast_fusion) | copy-start | bytes 10616836
  153.9 129.2 %copy-start.1 = (bf16[256,3,3,3,128]{4,0,3,2,1:T(8,128)(2,1)S(1)}, bf16[256,3,3,3,128]{4,0,3,2,1:T(8,128)(2,1)}, u32[]{:S(2)}) copy-start(bf16[256,3,3,3,128]{4,0,3,2,1:T(8,128)(2,1)} %param.10) | copy-start | bytes 5308420
Sparse Core Ops, SparseCore 0:
  35.3 7.4 reduce-scatter.3
  98.6 5.4 reduce-scatter.5
  154.0 126.9 reduce-scatter.7
where the time goes:
time: 291 us; the launch traced here: 290 us
  waiting for transfers between devices  127 us (44%)
  blocking collectives  54.5 us (19%)
  local copies, waits for them, and re-layouts  54.4 us (19%)
  matrix products  14.5 us (5%)
  between operations  14.3 us (5%)
  starting transfers between devices  13.2 us (5%)
  other arithmetic  11.5 us (4%)
    reduce_scatter x1, waiting for transfers between devices, shards(): lax.psum_scatter(jnp.stack([term_one(start, lax.axis_size(('tm', 'space')...  104 us
    psum x3, blocking collectives, clip_totals(): return lax.psum(values, ('tm', 'space'))  54.5 us
    unnamed x73, local copies, waits for them, and re-layouts  21.3 us
    dot_general x2, local copies, waits for them, and re-layouts, term(): lax.dot_general(flat_active, flat_taps, (((0,), (0,)), ((), ())), preferr...  15.9 us
    ppermute x2, waiting for transfers between devices, passed_along(): return lax.ppermute(block, axis, route)  14.5 us
    another operation x4, local copies, waits for them, and re-layouts, tap_stack(): stacked = jnp.stack(pieces, axis=3)  10.6 us
    dot_general x2, matrix products, term(): lax.dot_general(flat_active, flat_taps, (((0,), (0,)), ((), ())), preferr...  10.3 us
    ppermute x2, waiting for transfers between devices, extended_2(): lax.ppermute(head, axis, [((i + 1) % count, i) for i in range(ends)])  8.45 us
  transfers between devices with their start and end apart: 9, of which 7 were waited for; matrix products, arithmetic and copies ran while one was open for 22% of the time, Pallas kernels for 0%

commit v1 on v0

--- a/solution.py
+++ b/solution.py
@@ -31,7 +31,7 @@
 
 
 def clip_totals(values):
-    return lax.psum(values, ("tm", "space"))
+    return jnp.sum(lax.all_gather(values, ("tm", "space")), axis=0)
 
 
 def statistics(total, square, members, per):

time: 291 us -> 302 us (1.038)
  blocking collectives: 54.5 us -> 64.7 us
    all_gather x0 -> x3, blocking collectives: none -> 64.7 us  [clip_totals(): return jnp.sum(lax.all_gather(values, ('tm', 'space')), axis=0)]
    psum x3 -> x0, blocking collectives: 54.5 us -> none  [clip_totals(): return lax.psum(values, ('tm', 'space'))]
  transfers between devices with their start and end apart: 9 -> 9, of which waited for: 7 -> 7; matrix products, arithmetic and copies ran while one was open for 22% -> 21% of each run, Pallas kernels for 0% -> 0%
where the time goes in v1:
time: 302 us; the launch traced here: 301 us
  waiting for transfers between devices  129 us (43%)
  blocking collectives  64.7 us (21%)
  local copies, waits for them, and re-layouts  54.4 us (18%)
  matrix products  14.5 us (5%)
  between operations  14.3 us (5%)
  starting transfers between devices  13.3 us (4%)
  other arithmetic  11.5 us (4%)
    reduce_scatter x1, waiting for transfers between devices, shards(): lax.psum_scatter(jnp.stack([term_one(start, lax.axis_size(('tm', 'space')...  105 us
    all_gather x3, blocking collectives, clip_totals(): return jnp.sum(lax.all_gather(values, ('tm', 'space')), axis=0)  64.7 us
    unnamed x73, local copies, waits for them, and re-layouts  21.3 us
    dot_general x2, local copies, waits for them, and re-layouts, term(): lax.dot_general(flat_active, flat_taps, (((0,), (0,)), ((), ())), preferr...  15.9 us
    ppermute x2, waiting for transfers between devices, passed_along(): return lax.ppermute(block, axis, route)  14.5 us
    another operation x4, local copies, waits for them, and re-layouts, tap_stack(): stacked = jnp.stack(pieces, axis=3)  10.6 us
    dot_general x2, matrix products, term(): lax.dot_general(flat_active, flat_taps, (((0,), (0,)), ((), ())), preferr...  10.3 us
    ppermute x2, waiting for transfers between devices, extended_2(): lax.ppermute(head, axis, [((i + 1) % count, i) for i in range(ends)])  8.45 us
  transfers between devices with their start and end apart: 9, of which 7 were waited for; matrix products, arithmetic and copies ran while one was open for 21% of the time, Pallas kernels for 0%

profile of v1, /device:TPU:0, one launch (start us, length us, event | category | flops | bytes accessed | tf_op | source)
XLA Modules:
  0.0 301.2 jit_solution(11042020559190191468)
XLA Ops:
  7.2 1.1 constant_dynamic-slice_fusion.2
  8.4 4.9 %collective-permute-start = (bf16[2,1,90,128]{3,2,1,0:T(8,128)(2,1)S(1)}, bf16[2,1,90,128]{3,2,1,0:T(8,128)(2,1)S(1)}, u32[]{:S(2)}, u32[]{:S(2)}) collective-permute-start(bf16[2,1,90,128]{3,2,1,0:T(8,128)(2,1)S(1)} %get-tuple-element.45), channel_id=1, source_target_pairs={{0,2},{1,3},{4,6},{5,7},{8,10},{9,11},{12,14},{13,15},{16,18},{17,... | collective-permute-start | bytes 138248 | tf_op jit(solution)/shard_map/ppermute | solution.py:18
  13.3 1.3 collective-permute-start.1
  15.1 4.2 %collective-permute-done.1 = bf16[2,1,90,128]{3,2,1,0:T(8,128)(2,1)S(1)} collective-permute-done((bf16[2,1,90,128]{3,2,1,0:T(8,128)(2,1)S(1)}, bf16[2,1,90,128]{3,2,1,0:T(8,128)(2,1)S(1)}, u32[]{:S(2)}, u32[]{:S(2)}) %collective-permute-start.1) | collective-permute-done | bytes 46112 | tf_op jit(solution)/shard_map/ppermute | solution.py:20
  19.3 1.3 collective-permute-start.2
  20.6 7.9 %collective-permute-done.2 = bf16[2,6,90,128]{3,2,1,0:T(8,128)(2,1)S(1)} collective-permute-done((bf16[2,6,90,128]{3,2,1,0:T(8,128)(2,1)S(1)}, bf16[2,6,90,128]{3,2,1,0:T(8,128)(2,1)S(1)}, u32[]{:S(2)}, u32[]{:S(2)}) %collective-permute-start.2) | collective-permute-done | bytes 276512 | tf_op jit(solution)/shard_map/ppermute | solution.py:30
  30.3 2.3 copy-done.3
  32.7 2.5 convolution_bitcast_fusion.2
  35.6 30.6 %all-gather.3 = f32[8,4,256]{2,1,0:T(4,128)S(1)} all-gather(f32[1,4,256]{2,1,0:T(4,128)S(1)} %maximum_bitcast_fusion), channel_id=2, replica_groups=mesh['clip'=2,'tm'=4,'space'=2,'chan'=2] {'tm','space'}, dimensions={0}, use_global_device_ids=true | all-gather | bytes 36864 | tf_op jit(solution)/shard_map/all_gather | solution.py:34
  67.1 1.0 multiply_convert_fusion
  68.1 1.2 fusion.40
  69.3 17.3 %all-gather.4 = f32[8,2,128]{2,1,0:T(2,128)S(1)} all-gather(f32[1,2,128]{2,1,0:T(2,128)S(1)} %maximum_bitcast_fusion.1), channel_id=3, replica_groups=mesh['clip'=2,'tm'=4,'space'=2,'chan'=2] {'tm','space'}, dimensions={0}, use_global_device_ids=true | all-gather | bytes 9216 | tf_op jit(solution)/shard_map/all_gather | solution.py:34
  87.5 2.9 collective-permute-start.3
  90.5 1.3 collective-permute-start.4
  92.2 4.3 %collective-permute-done.4 = bf16[2,1,90,128]{3,2,1,0:T(8,128)(2,1)S(1)} collective-permute-done((bf16[2,1,90,128]{3,2,1,0:T(8,128)(2,1)S(1)}, bf16[2,1,90,128]{3,2,1,0:T(8,128)(2,1)S(1)}, u32[]{:S(2)}, u32[]{:S(2)}) %collective-permute-start.4) | collective-permute-done | bytes 46112 | tf_op jit(solution)/shard_map/ppermute | solution.py:20
  96.5 1.3 collective-permute-start.5
  98.6 6.6 %collective-permute-done.5 = bf16[2,6,90,128]{3,2,1,0:T(8,128)(2,1)S(1)} collective-permute-done((bf16[2,6,90,128]{3,2,1,0:T(8,128)(2,1)S(1)}, bf16[2,6,90,128]{3,2,1,0:T(8,128)(2,1)S(1)}, u32[]{:S(2)}, u32[]{:S(2)}) %collective-permute-start.5) | collective-permute-done | bytes 276512 | tf_op jit(solution)/shard_map/ppermute | solution.py:30
  107.4 1.6 fusion.2
  111.0 4.6 %copy.109 = bf16[2,4,90,27,128]{4,3,2,1,0:T(8,128)(2,1)S(1)} copy(bf16[2,4,90,27,128]{4,2,3,1,0:T(8,128)(2,1)} %copy-done.3) | data formatting | bytes 9953280 | tf_op jit(solution)/shard_map/stack | solution.py:74
  115.6 7.3 %copy.146 = bf16[90,8,27,128]{3,1,2,0:T(8,128)(2,1)} copy(bf16[90,8,27,128]{3,2,1,0:T(8,128)(2,1)S(1)} %bitcast.263) | data formatting | bytes 9953280
  122.9 7.9 %copy.110 = bf16[3456,720]{1,0:T(8,128)(2,1)} copy(bf16[3456,720]{0,1:T(8,128)(2,1)} %bitcast.267) | data formatting | bytes 9953280 | tf_op jit(solution)/shard_map/dot_general | solution.py:83
  130.8 6.0 %convolution_bitcast_fusion = f32[256,1,3,3,3,128]{5,0,4,3,2,1:T(8,128)} fusion(bf16[3,3,3,128,720]{4,3,2,1,0:T(8,128)(2,1)} %bitcast.265, bf16[720,256,1,1,1]{1,0,2,3,4:T(8,128)(2,1)S(1)} %reshape.347), kind=kOutput, calls=%fused_computation.5 | convolution fusion | flops 1274019840 | bytes 8884224 | tf_op jit(solution)/shard_map/dot_general | solution.py:83
  136.8 5.8 %copy.106 = bf16[2,4,90,27,128]{4,3,2,1,0:T(8,128)(2,1)S(1)} copy(bf16[2,4,90,27,128]{4,2,1,0,3:T(8,128)(2,1)} %copy-done.4) | data formatting | bytes 9953280 | tf_op jit(solution)/shard_map/stack | solution.py:74
  142.6 7.3 %copy.147 = bf16[90,8,27,128]{3,1,2,0:T(8,128)(2,1)} copy(bf16[90,8,27,128]{3,2,1,0:T(8,128)(2,1)S(1)} %bitcast.264) | data formatting | bytes 9953280
  149.9 8.0 %copy.107 = bf16[3456,720]{1,0:T(8,128)(2,1)} copy(bf16[3456,720]{0,1:T(8,128)(2,1)} %bitcast.268) | data formatting | bytes 9953280 | tf_op jit(solution)/shard_map/dot_general | solution.py:83
  157.9 4.3 %convolution_bitcast_fusion.1 = f32[256,1,3,3,3,128]{5,0,4,3,2,1:T(8,128)S(1)} fusion(bf16[3,3,3,128,720]{4,3,2,1,0:T(8,128)(2,1)} %bitcast.266, bf16[720,256,1,1,1]{1,0,2,3,4:T(8,128)(2,1)S(1)} %reshape.346), kind=kOutput, calls=%fused_computation.6 | convolution fusion | flops 1274019840 | bytes 8884224 | tf_op jit(solution)/shard_map/dot_general | solution.py:83
  162.2 3.4 %pad_maximum_fusion = f32[256,2,3,3,3,128]{5,0,4,3,2,1:T(8,128)} fusion(f32[256,1,3,3,3,128]{5,0,4,3,2,1:T(8,128)S(1)} %copy-done.2, f32[256,1,3,3,3,128]{5,0,4,3,2,1:T(8,128)S(1)} %convolution_bitcast_fusion.1), kind=kLoop, calls=%fused_computation | loop fusion | flops 1769472 | bytes 14155776 | tf_op jit(solution)/shard_map/stack | solution.py:151
  165.7 2.0 fusion.39
  167.7 16.8 %all-gather.5 = f32[8,2,128]{2,1,0:T(2,128)S(1)} all-gather(f32[1,2,128]{2,1,0:T(2,128)S(1)} %maximum_bitcast_fusion.2), channel_id=4, replica_groups=mesh['clip'=2,'tm'=4,'space'=2,'chan'=2] {'tm','space'}, dimensions={0}, use_global_device_ids=true | all-gather | bytes 9216 | tf_op jit(solution)/shard_map/all_gather | solution.py:34
  185.4 1.1 add_convert_fusion
  187.8 104.8 %reduce-scatter.8.cloned.1.call-done = f32[32,2,3,3,3,128]{5,0,4,3,2,1:T(8,128)} async-done(((f32[256,2,3,3,3,128]{5,0,4,3,2,1:T(8,128)}), f32[32,2,3,3,3,128]{5,0,4,3,2,1:T(8,128)}) %reduce-scatter.8.cloned.1.call-update) | async-done | bytes 884752 | tf_op jit(solution)/shard_map/reduce_scatter | solution.py:150
  292.6 2.1 slice_bitcast_fusion
  (153 shorter events, 12.0 us)
Async XLA Ops:
  7.2 23.1 %copy-start = (bf16[256,3,3,3,128]{4,0,3,2,1:T(8,128)(2,1)S(1)}, bf16[256,3,3,3,128]{4,0,3,2,1:T(8,128)(2,1)}, u32[]{:S(2)}) copy-start(bf16[256,3,3,3,128]{4,0,3,2,1:T(8,128)(2,1)} %param.10) | copy-start | bytes 5308420
  7.2 60.9 %reduce-scatter.4.cloned.1.call-start = ((), (), s32[]{:S(2)}) async-start(), calls=%async_computation.3 | async-start | bytes 1179648 | tf_op jit(solution)/shard_map/reduce_scatter | solution.py:102
  8.4 6.6 %collective-permute-start = (bf16[2,1,90,128]{3,2,1,0:T(8,128)(2,1)S(1)}, bf16[2,1,90,128]{3,2,1,0:T(8,128)(2,1)S(1)}, u32[]{:S(2)}, u32[]{:S(2)}) collective-permute-start(bf16[2,1,90,128]{3,2,1,0:T(8,128)(2,1)S(1)} %get-tuple-element.45), channel_id=1, source_target_pairs={{0,2},{1,3},{4,6},{5,7},{8,10},{9,11},{12,14},{13,15},{16,18},{17,... | collective-permute-start | bytes 138248 | tf_op jit(solution)/shard_map/ppermute | solution.py:18
  13.3 6.0 %collective-permute-start.1 = (bf16[2,1,90,128]{3,2,1,0:T(8,128)(2,1)S(1)}, bf16[2,1,90,128]{3,2,1,0:T(8,128)(2,1)S(1)}, u32[]{:S(2)}, u32[]{:S(2)}) collective-permute-start(bf16[2,1,90,128]{3,2,1,0:T(8,128)(2,1)S(1)} %get-tuple-element.44), channel_id=1, source_target_pairs={{2,0},{3,1},{6,4},{7,5},{10,8},{11,9},{14,12},{15,13},{18,16},{19,... | collective-permute-start | bytes 138248 | tf_op jit(solution)/shard_map/ppermute | solution.py:20
  19.3 9.2 %collective-permute-start.2 = (bf16[2,6,90,128]{3,2,1,0:T(8,128)(2,1)S(1)}, bf16[2,6,90,128]{3,2,1,0:T(8,128)(2,1)S(1)}, u32[]{:S(2)}, u32[]{:S(2)}) collective-permute-start(bf16[2,6,90,128]{3,2,1,0:T(8,128)(2,1)S(1)} %constant_dynamic-update-slice_fusion), channel_id=1, source_target_pairs={{4,0},{8,4},{12,8},{5,1},{9,5},{13,9},{6,2},{10,6},{14,10},{7,3},{... | collective-permute-start | bytes 829448 | tf_op jit(solution)/shard_map/ppermute | solution.py:30
  30.3 2.3 copy-start.3
  30.3 4.9 %copy-start.7 = (bf16[2,4,90,256]{3,1,2,0:T(4,128)(2,1)S(1)}, bf16[2,4,90,256]{3,1,2,0:T(4,128)(2,1)}, u32[]{:S(2)}) copy-start(bf16[2,4,90,256]{3,1,2,0:T(4,128)(2,1)} %param.6) | copy-start | bytes 1105924
  32.7 2.7 copy-start.6
  32.7 34.4 %copy-start.9 = (f32[2,256]{1,0:T(2,128)S(1)}, f32[2,256]{1,0:T(2,128)}, u32[]{:S(2)}) copy-start(f32[2,256]{1,0:T(2,128)} %param.11) | copy-start | bytes 6148
  35.2 130.5 %reduce-scatter.6.cloned.1.call-start = ((), (), s32[]{:S(2)}) async-start(), calls=%async_computation.4 | async-start | bytes 1179648 | tf_op jit(solution)/shard_map/reduce_scatter | solution.py:102
  87.5 4.7 %collective-permute-start.3 = (bf16[2,1,90,128]{3,2,1,0:T(8,128)(2,1)S(1)}, bf16[2,1,90,128]{3,2,1,0:T(8,128)(2,1)S(1)}, u32[]{:S(2)}, u32[]{:S(2)}) collective-permute-start(bf16[2,1,90,128]{3,2,1,0:T(8,128)(2,1)S(1)} %get-tuple-element.42), channel_id=1, source_target_pairs={{0,2},{1,3},{4,6},{5,7},{8,10},{9,11},{12,14},{13,15},{16,18},{17,... | collective-permute-start | bytes 138248 | tf_op jit(solution)/shard_map/ppermute | solution.py:18
  90.5 6.0 %collective-permute-start.4 = (bf16[2,1,90,128]{3,2,1,0:T(8,128)(2,1)S(1)}, bf16[2,1,90,128]{3,2,1,0:T(8,128)(2,1)S(1)}, u32[]{:S(2)}, u32[]{:S(2)}) collective-permute-start(bf16[2,1,90,128]{3,2,1,0:T(8,128)(2,1)S(1)} %get-tuple-element.43), channel_id=1, source_target_pairs={{2,0},{3,1},{6,4},{7,5},{10,8},{11,9},{14,12},{15,13},{18,16},{19,... | collective-permute-start | bytes 138248 | tf_op jit(solution)/shard_map/ppermute | solution.py:20
  96.5 8.6 %collective-permute-start.5 = (bf16[2,6,90,128]{3,2,1,0:T(8,128)(2,1)S(1)}, bf16[2,6,90,128]{3,2,1,0:T(8,128)(2,1)S(1)}, u32[]{:S(2)}, u32[]{:S(2)}) collective-permute-start(bf16[2,6,90,128]{3,2,1,0:T(8,128)(2,1)S(1)} %pad_maximum_fusion.3), channel_id=1, source_target_pairs={{4,0},{8,4},{12,8},{5,1},{9,5},{13,9},{6,2},{10,6},{14,10},{7,3},{... | collective-permute-start | bytes 829448 | tf_op jit(solution)/shard_map/ppermute | solution.py:30
  105.9 1.5 copy-start.10
  106.9 2.3 copy-start.4
  107.4 3.1 %copy-start.8 = (bf16[2,4,90,256]{3,1,2,0:T(4,128)(2,1)S(1)}, bf16[2,4,90,256]{3,1,2,0:T(4,128)(2,1)}, u32[]{:S(2)}) copy-start(bf16[2,4,90,256]{3,1,2,0:T(4,128)(2,1)} %param.6) | copy-start | bytes 1105924
  109.2 1.6 copy-start.5
  110.2 182.4 %reduce-scatter.8.cloned.1.call-start = ((), (), s32[]{:S(2)}) async-start(), calls=%async_computation.5 | async-start | bytes 7962624 | tf_op jit(solution)/shard_map/reduce_scatter | solution.py:150
  157.9 4.3 %copy-start.2 = (f32[256,1,3,3,3,128]{5,0,4,3,2,1:T(8,128)S(1)}, f32[256,1,3,3,3,128]{5,0,4,3,2,1:T(8,128)}, u32[]{:S(2)}) copy-start(f32[256,1,3,3,3,128]{5,0,4,3,2,1:T(8,128)} %convolution_bitcast_fusion) | copy-start | bytes 10616836
  165.6 129.1 %copy-start.1 = (bf16[256,3,3,3,128]{4,0,3,2,1:T(8,128)(2,1)S(1)}, bf16[256,3,3,3,128]{4,0,3,2,1:T(8,128)(2,1)}, u32[]{:S(2)}) copy-start(bf16[256,3,3,3,128]{4,0,3,2,1:T(8,128)(2,1)} %param.10) | copy-start | bytes 5308420
Sparse Core Ops, SparseCore 0:
  35.3 7.4 reduce-scatter.3
  110.4 5.4 reduce-scatter.5
  165.7 126.8 reduce-scatter.7
